TPU v7x, 256 devices: a whole 4x4x8 slice. The times are simulated.
256 devices in a mesh: grp: 4 (over z_hi), freq: 64 (over z_lo, y, x, core).
Axes of the slice: x: 4, y: 4, z: 8 (z_hi: 4, z_lo: 2; z = z_hi * 2 + z_lo), core: 2. Of those that a mesh axis runs over, the one named last changes fastest.
Arguments:
- sources: bfloat16 [1024, 262144], P('freq', 'grp'), may hold values from -6 to 6
- panel_pos: float32 [3, 262144], P(None, 'grp'), may hold values from -1 to 1
- panel_blade: int32 [262144], P('grp'), may hold values from 0 to 3
- observer_table: float32 [3, 2048], replicated, may hold values from -8 to 8, as said below
- observer_index: int32 [32], replicated, may hold values from 0 to 2047
Outputs:
- spectra: float32 [512, 4, 2, 32], P('freq', 'grp')
Inputs may be any that keep to these rules, and one draw needn't show every extreme that they name: `observer_table`: each observer lies 3 to 8 units from the anchor (0, 0, 0).
All inputs are finite; a program needn't handle non-finite values.
Results may differ from a plain program's by a relative error of at most 0.0047.
Values may be sent and summed in bfloat16 or wider, within the bound.
A program may use at most 64 MiB of HBM per device.

v0:
```python
import math

import jax
import jax.numpy as jnp
from jax import lax
from jax.sharding import PartitionSpec as P

NT = 1024
NF = 512
NCOMP = 4


wave_step = 0.04


def over_pieces(x, axis):
    return lax.all_gather(x, axis).sum(0)


def transform_table():
    row_index = jnp.arange(2 * NF, dtype=jnp.int32)
    samples = jnp.arange(NT, dtype=jnp.int32)
    frequency = row_index // 2
    parity = row_index % 2
    turn_count = frequency[:, None] * samples[None, :] % NT
    angle_table = 2.0 * math.pi / NT * turn_count.astype(jnp.float32)
    values = jnp.where(parity[:, None] == 0, jnp.cos(angle_table), -jnp.sin(angle_table))
    return (values / math.sqrt(NT)).astype(jnp.bfloat16)


def distances(positions, observers):
    offset_x = observers[0][:, None] - positions[0][None, :]
    offset_y = observers[1][:, None] - positions[1][None, :]
    offset_z = observers[2][:, None] - positions[2][None, :]
    return jnp.sqrt(offset_x * offset_x + offset_y * offset_y + offset_z * offset_z)


def blade_masks(blades):
    return (blades[None, :] == jnp.arange(NCOMP, dtype=jnp.int32)[:, None]).astype(jnp.bfloat16)


def frequency_term(frequency, spectrum_pair, blade_mask, distance, amplitude):
    wavenumber = wave_step * frequency.astype(jnp.float32)
    phase_angle = wavenumber * distance
    green_matrix = jnp.concatenate(
        [jnp.cos(phase_angle) * amplitude, -jnp.sin(phase_angle) * amplitude], axis=0
    ).astype(jnp.bfloat16)
    weighted = jnp.concatenate(
        [spectrum_pair[0][None, :] * blade_mask, spectrum_pair[1][None, :] * blade_mask], axis=0
    )
    product = lax.dot_general(
        weighted, green_matrix, (((1,), (1,)), ((), ())), preferred_element_type=jnp.float32
    )
    blade_count = blade_mask.shape[0]
    observer_count = distance.shape[0]
    real_part = product[:blade_count, :observer_count] - product[blade_count:, observer_count:]
    imag_part = product[:blade_count, observer_count:] + product[blade_count:, :observer_count]
    return jnp.stack([real_part, imag_part], axis=1)


def body(sources, panel_pos, panel_blade, observer_table, observer_index):
    freq_share = NF // lax.axis_size("freq")
    position = lax.axis_index("freq")
    observers = observer_table[:, observer_index]
    dft_table = transform_table()
    exchanged = lax.all_to_all(sources, "freq", split_axis=1, concat_axis=0, tiled=True)
    spectrum = jnp.dot(dft_table, exchanged, preferred_element_type=jnp.float32).astype(
        jnp.bfloat16
    )
    received = lax.all_to_all(spectrum, "freq", split_axis=0, concat_axis=1, tiled=True)
    spectra_pairs = received.reshape(freq_share, 2, received.shape[1])
    distance = distances(panel_pos, observers)
    amplitude = 0.25 / (math.pi * distance)
    blade_mask = blade_masks(panel_blade)
    frequencies = position * freq_share + jnp.arange(freq_share, dtype=jnp.int32)

    def per_frequency(element):
        return frequency_term(element[0], element[1], blade_mask, distance, amplitude)

    partial_value = lax.map(per_frequency, (frequencies, spectra_pairs))
    summed = over_pieces(partial_value, "grp")
    blade_share = NCOMP // lax.axis_size("grp")
    return lax.dynamic_slice_in_dim(summed, lax.axis_index("grp") * blade_share, blade_share, 1)


def solution(mesh):
    in_specs = (P("freq", "grp"), P(None, "grp"), P("grp"), P(), P())
    out_specs = P("freq", "grp", None, None)
    return jax.shard_map(body, mesh=mesh, in_specs=in_specs, out_specs=out_specs, check_vma=False)
```

profile of v0, /device:TPU:1, one launch (start us, length us, event | category | flops | bytes accessed | tf_op | source)
XLA Modules:
  0.0 449.2 jit_solution(7879830638706427243)
XLA Ops:
  0.0 3.2 copy.19
  3.2 10.3 %all-to-all-start = ((bf16[16,64,1024]{2,0,1:T(8,128)(2,1)}), bf16[16,64,1024]{2,0,1:T(8,128)(2,1)S(1)}, u32[]{:S(2)}, u32[]{:S(2)}) async-start(bf16[16,64,1024]{2,0,1:T(8,128)(2,1)} %bitcast.24), calls=%async_computation | async-start | bytes 4194304 | tf_op jit(solution)/shard_map/all_to_all | solution.py:66
  13.5 27.5 %all-to-all-done = bf16[16,64,1024]{2,0,1:T(8,128)(2,1)S(1)} async-done(((bf16[16,64,1024]{2,0,1:T(8,128)(2,1)}), bf16[16,64,1024]{2,0,1:T(8,128)(2,1)S(1)}, u32[]{:S(2)}, u32[]{:S(2)}) %all-to-all-start) | async-done | bytes 2097184 | tf_op jit(solution)/shard_map/all_to_all | solution.py:66
  41.1 21.4 %fusion.32 = bf16[1024,1024]{1,0:T(8,128)(2,1)} fusion(bf16[1024,1024]{1,0:T(8,128)(2,1)S(1)} %bitcast.34, s32[1024]{0:T(1024)S(1)} %add_select_fusion.1, pred[1024]{0:T(1024)(128)(4,1)S(1)} %fusion.33), kind=kOutput, calls=%fused_computation.45 | convolution fusion | flops 2167406592 | bytes 4199424 | tf_op jit(solution)/shard_map/dot_general | solution.py:67
  62.4 7.6 %all-to-all-start.1 = ((bf16[64,16,1024]{2,1,0:T(8,128)(2,1)}), bf16[64,16,1024]{2,1,0:T(8,128)(2,1)S(1)}, u32[]{:S(2)}, u32[]{:S(2)}) async-start(bf16[64,16,1024]{2,1,0:T(8,128)(2,1)} %bitcast.33), calls=%async_computation.1 | async-start | bytes 4194304 | tf_op jit(solution)/shard_map/all_to_all | solution.py:70
  70.1 1.4 fusion.44
  71.5 0.4 copy.15
  72.0 0.6 gather_fusion
  72.5 0.2 slice_reduce_fusion
  72.8 24.9 %all-to-all-done.1 = bf16[64,16,1024]{2,1,0:T(8,128)(2,1)S(1)} async-done(((bf16[64,16,1024]{2,1,0:T(8,128)(2,1)}), bf16[64,16,1024]{2,1,0:T(8,128)(2,1)S(1)}, u32[]{:S(2)}, u32[]{:S(2)}) %all-to-all-start.1) | async-done | bytes 2097184 | tf_op jit(solution)/shard_map/all_to_all | solution.py:70
  97.6 2.5 copy.14
  100.1 4.9 %reshape.45 = bf16[8,2,65536]{2,1,0:T(2,128)(2,1)S(1)} reshape(bf16[16,64,1024]{2,1,0:T(8,128)(2,1)} %copy.14) | data formatting | bytes 4194304 | tf_op jit(solution)/shard_map/reshape | solution.py:71
  105.0 0.0 copy-done
  105.1 329.8 %while.12 = (s32[]{:T(128)}, f32[8,4,2,32]{3,1,2,0:T(4,128)S(1)}, bf16[8,2,65536]{2,1,0:T(2,128)(2,1)S(1)}, s32[8]{0:T(128)S(1)}, s32[65536]{0:T(1024)S(1)}, /*i...) while((s32[]{:T(128)}, f32[8,4,2,32]{3,1,2,0:T(4,128)S(1)}, ...), condition=%wide.region_1.2_spmd.clone.clone, body=%wide.region_0.1_spmd.clone.clone.sunk | while | flops 120324608 | bytes 20723280 | solution.py:80
  105.1 0.6 dynamic_slice.18
  106.2 1.4 dynamic-slice_reduce_fusion.3
  107.6 0.5 fusion.53
  108.1 35.8 %multiply_convert_fusion.7 = (bf16[32,65536]{1,0:T(8,128)(2,1)S(1)}, bf16[32,65536]{1,0:T(8,128)(2,1)S(1)}) fusion(f32[65536]{0:T(1024)S(1)} %get-tuple-element.290, f32[32]{0:T(128)S(1)} %get-tuple-element.291, f32[65536]{0:T(1024)S(1)} %get-tuple-element.288, f32[32]{0:T(128)S(1)} %get-tuple-element.289, f32[65536]{0:T(1024)S(1)} %get-tuple-element.286, ...), kind=kLoop, calls=%fused_computation.11.clone.1 | loop fusion | flops 33554432 | bytes 9175428 | tf_op jit(solution)/shard_map/convert
  143.9 2.3 fusion.54
  146.2 0.1 subtract_bitcast_fusion.2
  146.3 0.6 dynamic_slice.18
  147.4 1.4 dynamic-slice_reduce_fusion.3
  148.9 0.5 fusion.53
  149.3 35.8 %multiply_convert_fusion.7 = (bf16[32,65536]{1,0:T(8,128)(2,1)S(1)}, bf16[32,65536]{1,0:T(8,128)(2,1)S(1)}) fusion(f32[65536]{0:T(1024)S(1)} %get-tuple-element.290, f32[32]{0:T(128)S(1)} %get-tuple-element.291, f32[65536]{0:T(1024)S(1)} %get-tuple-element.288, f32[32]{0:T(128)S(1)} %get-tuple-element.289, f32[65536]{0:T(1024)S(1)} %get-tuple-element.286, ...), kind=kLoop, calls=%fused_computation.11.clone.1 | loop fusion | flops 33554432 | bytes 9175428 | tf_op jit(solution)/shard_map/convert
  185.1 2.3 fusion.54
  187.4 0.1 subtract_bitcast_fusion.2
  187.5 0.6 dynamic_slice.18
  188.7 1.4 dynamic-slice_reduce_fusion.3
  190.1 0.5 fusion.53
  190.6 35.8 %multiply_convert_fusion.7 = (bf16[32,65536]{1,0:T(8,128)(2,1)S(1)}, bf16[32,65536]{1,0:T(8,128)(2,1)S(1)}) fusion(f32[65536]{0:T(1024)S(1)} %get-tuple-element.290, f32[32]{0:T(128)S(1)} %get-tuple-element.291, f32[65536]{0:T(1024)S(1)} %get-tuple-element.288, f32[32]{0:T(128)S(1)} %get-tuple-element.289, f32[65536]{0:T(1024)S(1)} %get-tuple-element.286, ...), kind=kLoop, calls=%fused_computation.11.clone.1 | loop fusion | flops 33554432 | bytes 9175428 | tf_op jit(solution)/shard_map/convert
  226.4 2.3 fusion.54
  228.6 0.1 subtract_bitcast_fusion.2
  228.7 0.6 dynamic_slice.18
  229.9 1.4 dynamic-slice_reduce_fusion.3
  231.3 0.5 fusion.53
  231.8 35.8 %multiply_convert_fusion.7 = (bf16[32,65536]{1,0:T(8,128)(2,1)S(1)}, bf16[32,65536]{1,0:T(8,128)(2,1)S(1)}) fusion(f32[65536]{0:T(1024)S(1)} %get-tuple-element.290, f32[32]{0:T(128)S(1)} %get-tuple-element.291, f32[65536]{0:T(1024)S(1)} %get-tuple-element.288, f32[32]{0:T(128)S(1)} %get-tuple-element.289, f32[65536]{0:T(1024)S(1)} %get-tuple-element.286, ...), kind=kLoop, calls=%fused_computation.11.clone.1 | loop fusion | flops 33554432 | bytes 9175428 | tf_op jit(solution)/shard_map/convert
  267.6 2.3 fusion.54
  269.8 0.1 subtract_bitcast_fusion.2
  269.9 0.6 dynamic_slice.18
  271.1 1.4 dynamic-slice_reduce_fusion.3
  272.5 0.5 fusion.53
  273.0 35.8 %multiply_convert_fusion.7 = (bf16[32,65536]{1,0:T(8,128)(2,1)S(1)}, bf16[32,65536]{1,0:T(8,128)(2,1)S(1)}) fusion(f32[65536]{0:T(1024)S(1)} %get-tuple-element.290, f32[32]{0:T(128)S(1)} %get-tuple-element.291, f32[65536]{0:T(1024)S(1)} %get-tuple-element.288, f32[32]{0:T(128)S(1)} %get-tuple-element.289, f32[65536]{0:T(1024)S(1)} %get-tuple-element.286, ...), kind=kLoop, calls=%fused_computation.11.clone.1 | loop fusion | flops 33554432 | bytes 9175428 | tf_op jit(solution)/shard_map/convert
  308.8 2.3 fusion.54
  311.1 0.1 subtract_bitcast_fusion.2
  311.2 0.6 dynamic_slice.18
  312.3 1.4 dynamic-slice_reduce_fusion.3
  313.7 0.5 fusion.53
  314.2 35.8 %multiply_convert_fusion.7 = (bf16[32,65536]{1,0:T(8,128)(2,1)S(1)}, bf16[32,65536]{1,0:T(8,128)(2,1)S(1)}) fusion(f32[65536]{0:T(1024)S(1)} %get-tuple-element.290, f32[32]{0:T(128)S(1)} %get-tuple-element.291, f32[65536]{0:T(1024)S(1)} %get-tuple-element.288, f32[32]{0:T(128)S(1)} %get-tuple-element.289, f32[65536]{0:T(1024)S(1)} %get-tuple-element.286, ...), kind=kLoop, calls=%fused_computation.11.clone.1 | loop fusion | flops 33554432 | bytes 9175428 | tf_op jit(solution)/shard_map/convert
  350.0 2.3 fusion.54
  352.3 0.1 subtract_bitcast_fusion.2
  352.4 0.6 dynamic_slice.18
  353.5 1.4 dynamic-slice_reduce_fusion.3
  355.0 0.5 fusion.53
  355.5 35.8 %multiply_convert_fusion.7 = (bf16[32,65536]{1,0:T(8,128)(2,1)S(1)}, bf16[32,65536]{1,0:T(8,128)(2,1)S(1)}) fusion(f32[65536]{0:T(1024)S(1)} %get-tuple-element.290, f32[32]{0:T(128)S(1)} %get-tuple-element.291, f32[65536]{0:T(1024)S(1)} %get-tuple-element.288, f32[32]{0:T(128)S(1)} %get-tuple-element.289, f32[65536]{0:T(1024)S(1)} %get-tuple-element.286, ...), kind=kLoop, calls=%fused_computation.11.clone.1 | loop fusion | flops 33554432 | bytes 9175428 | tf_op jit(solution)/shard_map/convert
  391.2 2.3 fusion.54
  393.5 0.1 subtract_bitcast_fusion.2
  393.6 0.6 dynamic_slice.18
  394.8 1.4 dynamic-slice_reduce_fusion.3
  396.2 0.5 fusion.53
  396.7 35.8 %multiply_convert_fusion.7 = (bf16[32,65536]{1,0:T(8,128)(2,1)S(1)}, bf16[32,65536]{1,0:T(8,128)(2,1)S(1)}) fusion(f32[65536]{0:T(1024)S(1)} %get-tuple-element.290, f32[32]{0:T(128)S(1)} %get-tuple-element.291, f32[65536]{0:T(1024)S(1)} %get-tuple-element.288, f32[32]{0:T(128)S(1)} %get-tuple-element.289, f32[65536]{0:T(1024)S(1)} %get-tuple-element.286, ...), kind=kLoop, calls=%fused_computation.11.clone.1 | loop fusion | flops 33554432 | bytes 9175428 | tf_op jit(solution)/shard_map/convert
  432.5 2.3 fusion.54
  434.7 0.1 subtract_bitcast_fusion.2
  434.8 13.7 %all-gather = f32[32,4,2,32]{3,1,2,0:T(4,128)S(1)} all-gather(f32[8,4,2,32]{3,1,2,0:T(4,128)S(1)} %get-tuple-element.42), channel_id=2, replica_groups=mesh['grp'=4,'freq'=64] {'grp'}, dimensions={0}, use_global_device_ids=true | all-gather | bytes 40960 | tf_op jit(solution)/shard_map/all_gather | solution.py:17
  448.5 0.6 constant_dynamic-slice_fusion
  (28 shorter events, 0.2 us)
Async XLA Ops:
  3.2 37.9 %all-to-all-start = ((bf16[16,64,1024]{2,0,1:T(8,128)(2,1)}), bf16[16,64,1024]{2,0,1:T(8,128)(2,1)S(1)}, u32[]{:S(2)}, u32[]{:S(2)}) async-start(bf16[16,64,1024]{2,0,1:T(8,128)(2,1)} %bitcast.24), calls=%async_computation | async-start | bytes 4194304 | tf_op jit(solution)/shard_map/all_to_all | solution.py:66
  62.4 7.7 %copy-start.1 = (f32[3,65536]{1,0:T(4,128)S(1)}, f32[3,65536]{1,0:T(4,128)}, u32[]{:S(2)}) copy-start(f32[3,65536]{1,0:T(4,128)} %param.8) | copy-start | bytes 2359300
  62.4 9.1 %copy-start.5 = (f32[3,2048]{1,0:T(4,128)S(1)}, f32[3,2048]{1,0:T(4,128)}, u32[]{:S(2)}) copy-start(f32[3,2048]{1,0:T(4,128)} %param.10) | copy-start | bytes 73732
  62.4 9.5 %copy-start.6 = (s32[32]{0:T(128)S(1)}, s32[32]{0:T(128)}, u32[]{:S(2)}) copy-start(s32[32]{0:T(128)} %param.11) | copy-start | bytes 388
  62.4 35.2 %all-to-all-start.1 = ((bf16[64,16,1024]{2,1,0:T(8,128)(2,1)}), bf16[64,16,1024]{2,1,0:T(8,128)(2,1)S(1)}, u32[]{:S(2)}, u32[]{:S(2)}) async-start(bf16[64,16,1024]{2,1,0:T(8,128)(2,1)} %bitcast.33), calls=%async_computation.1 | async-start | bytes 4194304 | tf_op jit(solution)/shard_map/all_to_all | solution.py:70
  97.6 7.4 %copy-start = (s32[65536]{0:T(1024)S(1)}, s32[65536]{0:T(1024)}, u32[]{:S(2)}) copy-start(s32[65536]{0:T(1024)} %param.9) | copy-start | bytes 786436
  97.6 7.4 %copy-start.2 = (f32[1,65536]{1,0:T(1,128)S(1)}, f32[1,65536]{1,0:T(1,128)}, u32[]{:S(2)}) copy-start(f32[1,65536]{1,0:T(1,128)} %get-tuple-element.165) | copy-start | bytes 786436
  97.6 7.4 %copy-start.3 = (f32[1,65536]{1,0:T(1,128)S(1)}, f32[1,65536]{1,0:T(1,128)}, u32[]{:S(2)}) copy-start(f32[1,65536]{1,0:T(1,128)} %get-tuple-element.166) | copy-start | bytes 786436
  97.6 7.4 %copy-start.4 = (f32[1,65536]{1,0:T(1,128)S(1)}, f32[1,65536]{1,0:T(1,128)}, u32[]{:S(2)}) copy-start(f32[1,65536]{1,0:T(1,128)} %get-tuple-element.167) | copy-start | bytes 786436
where the time goes:
time: 452 us; the launch traced here: 449 us
  other arithmetic  291 us (64%)
  waiting for transfers between devices  52.4 us (12%)
  matrix products  39.5 us (9%)
  local copies, waits for them, and re-layouts  29.8 us (7%)
  starting transfers between devices  18 us (4%)
  blocking collectives  13.7 us (3%)
  loops' own time  4.72 us (1%)
    another operation x8, other arithmetic  286 us
    all_to_all x1, waiting for transfers between devices, body(): lax.all_to_all(sources, 'freq', split_axis=1, concat_axis=0, tiled=True)  27.5 us
    all_to_all x1, waiting for transfers between devices, body(): lax.all_to_all(spectrum, 'freq', split_axis=0, concat_axis=1, tiled=True)  24.9 us
    dot_general x1, matrix products, body(): jnp.dot(dft_table, exchanged, preferred_element_type=jnp.float32)  21.4 us
    dot_general x8, matrix products, frequency_term(): lax.dot_general(weighted, green_matrix, (((1,), (1,)), ((), ())), preferr...  18.1 us
    all_gather x1, blocking collectives, over_pieces(): return lax.all_gather(x, axis).sum(0)  13.7 us
    slice x8, local copies, waits for them, and re-layouts, frequency_term(): spectrum_pair[0][None, :] * blade_mask  11.3 us
    all_to_all x1, starting transfers between devices, body(): lax.all_to_all(sources, 'freq', split_axis=1, concat_axis=0, tiled=True)  10.3 us
  transfers between devices with their start and end apart: 2, of which 2 were waited for; matrix products, arithmetic and copies ran while one was open for 1% of the time, Pallas kernels for 0%

commit v1 on v0

v1 whole, which is shorter than its diff:
```python
import functools
import math

import jax
import jax.numpy as jnp
from jax import lax
from jax.experimental import pallas as pl
from jax.experimental.pallas import tpu as pltpu
from jax.sharding import PartitionSpec as P

NT = 1024
NF = 512
NCOMP = 4
NOBS = 32

wave_step = 0.04

FREQ_RANKS = 64
GRP_RANKS = 4
ROWS = NT // FREQ_RANKS
CHUNKS = 4
WIDTH = 256
SHARE = CHUNKS * WIDTH
JOINT = 4
TILES = NF // JOINT
UNROLL = 16
STEPS = TILES // UNROLL
MESH = pl.DeviceIdType.MESH


def transform_table():
    row_index = jnp.arange(2 * NF, dtype=jnp.int32)
    samples = jnp.arange(NT, dtype=jnp.int32)
    frequency = row_index // 8 * JOINT + row_index % JOINT
    parity = row_index // JOINT % 2
    turn_count = frequency[:, None] * samples[None, :] % NT
    angle_table = 2.0 * math.pi / NT * turn_count.astype(jnp.float32)
    values = jnp.where(parity[:, None] == 0, jnp.cos(angle_table), -jnp.sin(angle_table))
    return (values / math.sqrt(NT)).astype(jnp.bfloat16)


def partner(me, i):
    e = i * 37 % FREQ_RANKS
    core = (me + e) % 2
    x = (me // 2 + e // 2) % 4
    y = (me // 8 + e // 8) % 4
    z = (me // 32 + e // 32) % 2
    return z * 32 + y * 8 + x * 2 + core


def kernel(
    source_hbm, table_hbm, panel_ref, observer_ref, out_ref,
    source, table, received, state, green, weighted, total, partial, gathered, share_out, share_in,
    load_sem, table_sem, send_sem, recv_sem, sum_send, sum_recv, share_send, share_recv,
):
    me = lax.axis_index("freq")
    group = lax.axis_index("grp")
    load = pltpu.make_async_copy(source_hbm, source, load_sem)
    load.start()
    table_load = pltpu.make_async_copy(table_hbm, table, table_sem)
    table_load.start()

    barrier = pltpu.get_barrier_semaphore()

    def greet(i, carry):
        pl.semaphore_signal(
            barrier, inc=1, device_id={"freq": partner(me, i)}, device_id_type=MESH
        )
        return carry

    lax.fori_loop(1, FREQ_RANKS, greet, 0)
    for i in range(1, GRP_RANKS):
        pl.semaphore_signal(
            barrier, inc=1, device_id={"grp": (group + i) % GRP_RANKS}, device_id_type=MESH
        )
    load.wait()
    pl.semaphore_wait(barrier, FREQ_RANKS - 1 + GRP_RANKS - 1)

    own_rows = pl.ds(pl.multiple_of(me * ROWS, ROWS), ROWS)

    def columns(device, chunk):
        return pl.ds(pl.multiple_of(device * SHARE + chunk * WIDTH, WIDTH), WIDTH)

    for chunk in range(CHUNKS):

        def send(i, carry):
            device = partner(me, i)
            pltpu.make_async_remote_copy(
                src_ref=source.at[:, columns(device, chunk)],
                dst_ref=received.at[chunk, own_rows, :],
                send_sem=send_sem.at[chunk],
                recv_sem=recv_sem.at[chunk],
                device_id={"freq": device},
                device_id_type=MESH,
            ).start()
            return carry

        pltpu.make_async_copy(
            source.at[:, columns(me, chunk)],
            received.at[chunk, own_rows, :],
            recv_sem.at[chunk],
        ).start()
        lax.fori_loop(1, FREQ_RANKS, send, 0)

    def seed(chunk):
        for half in range(WIDTH // 128):
            squares = None
            for axis in range(3):
                row = panel_ref[axis : axis + 1, pl.ds(chunk * WIDTH + half * 128, 128)]
                column = jnp.broadcast_to(row, (128, 128)).T
                offset = observer_ref[axis : axis + 1, :] - column
                squares = offset * offset if squares is None else squares + offset * offset
            inverse = lax.rsqrt(squares)
            distance = squares * inverse
            amplitude = (0.25 / math.pi) * inverse
            angle = wave_step * distance
            w = angle * angle
            cos1 = 1.0 + w * (-1 / 2 + w * (1 / 24 + w * (-1 / 720 + w * (1 / 40320 - w * (1 / 3628800)))))
            sin1 = angle * (1.0 + w * (-1 / 6 + w * (1 / 120 + w * (-1 / 5040 + w * (1 / 362880)))))
            cos2 = cos1 * cos1 - sin1 * sin1
            sin2 = 2.0 * sin1 * cos1
            cos3 = cos2 * cos1 - sin2 * sin1
            sin3 = sin2 * cos1 + cos2 * sin1
            cos4 = cos2 * cos2 - sin2 * sin2
            sin4 = 2.0 * sin2 * cos2
            lane = lax.broadcasted_iota(jnp.int32, (128, 128), 1) // NOBS
            cos_j = jnp.where(lane == 0, 1.0, jnp.where(lane == 1, cos1, jnp.where(lane == 2, cos2, cos3)))
            sin_j = jnp.where(lane == 0, 0.0, jnp.where(lane == 1, sin1, jnp.where(lane == 2, sin2, sin3)))
            rows = pl.ds(half * 128, 128)
            state[0, rows, :] = 2.0 * cos4
            state[1, rows, :] = amplitude * (cos_j * cos4 + sin_j * sin4)
            state[2, rows, :] = amplitude * cos_j
            state[3, rows, :] = -amplitude * (sin_j * cos4 - cos_j * sin4)
            state[4, rows, :] = -amplitude * sin_j

    def grow(slot, step):
        for block in range(WIDTH // 16):
            rows = pl.ds(block * 16, 16)
            twice = state[0, rows, :]
            re_old, re_new = state[1, rows, :], state[2, rows, :]
            im_old, im_new = state[3, rows, :], state[4, rows, :]
            for u in range(UNROLL):
                tile = step * UNROLL + u
                green[slot, tile, rows, 0:128] = re_new.astype(jnp.bfloat16)
                green[slot, tile, rows, 128:256] = im_new.astype(jnp.bfloat16)
                re_old, re_new = re_new, twice * re_new - re_old
                im_old, im_new = im_new, twice * im_new - im_old
            state[1, rows, :] = re_old
            state[2, rows, :] = re_new
            state[3, rows, :] = im_old
            state[4, rows, :] = im_new

    def grow_all(slot):
        lax.fori_loop(0, STEPS, lambda step, c: (grow(slot, step), c)[1], 0)

    seed(0)
    grow_all(0)
    seed(1)
    grow_all(1)
    table_load.wait()

    sublane = lax.broadcasted_iota(jnp.int32, (8, 128), 0)
    lane_joint = lax.broadcasted_iota(jnp.int32, (8, 128), 1) // NOBS
    keep_a = (sublane == lane_joint).astype(jnp.float32)
    keep_c = (sublane == lane_joint + JOINT).astype(jnp.float32)

    def transform(chunk):
        blades = panel_ref[3:4, pl.ds(chunk * WIDTH, WIDTH)]
        masks = [(blades == float(b)).astype(jnp.float32).reshape(1, 1, WIDTH) for b in range(NCOMP)]

        def part(i, carry):
            spectrum = jnp.dot(
                table[pl.ds(pl.multiple_of(i * 256, 256), 256), :],
                received[chunk],
                preferred_element_type=jnp.float32,
            ).reshape(32, 8, WIDTH)
            for pair in range(NCOMP // 2):
                both = jnp.concatenate([spectrum * masks[2 * pair], spectrum * masks[2 * pair + 1]], axis=1)
                weighted[pl.ds(i * 32, 32), pl.ds(16 * pair, 16), :] = both.astype(jnp.bfloat16)
            return carry

        lax.fori_loop(0, 4, part, 0)

    def pressure(value):
        sums = []
        for blade in range(NCOMP):
            re_side = value[8 * blade : 8 * blade + 8, 0:128]
            im_side = value[8 * blade : 8 * blade + 8, 128:256]
            sums.append(jnp.sum(re_side * keep_a - im_side * keep_c, axis=0, keepdims=True))
            sums.append(jnp.sum(im_side * keep_a + re_side * keep_c, axis=0, keepdims=True))
        return jnp.concatenate(sums, axis=0)

    def send_sums(step):
        for u in range(UNROLL // 2):
            device = step * (UNROLL // 2) + u

            @pl.when(device != me)
            def _():
                pltpu.make_async_remote_copy(
                    src_ref=partial.at[device],
                    dst_ref=gathered.at[me],
                    send_sem=sum_send,
                    recv_sem=sum_recv,
                    device_id={"freq": device},
                    device_id_type=MESH,
                ).start()

    for chunk in range(CHUNKS):
        pltpu.make_async_copy(received.at[chunk], received.at[chunk], recv_sem.at[chunk]).wait()
        transform(chunk)
        slot = chunk % 2
        ahead = chunk + 2 < CHUNKS
        last = chunk == CHUNKS - 1
        if ahead:
            seed(chunk + 2)

        def contract(step, carry):
            if last:

                @pl.when(step > 0)
                def _():
                    send_sums(step - 1)

            rows = []
            for u in range(UNROLL):
                tile = step * UNROLL + u
                product = jnp.dot(weighted[tile], green[slot, tile], preferred_element_type=jnp.float32)
                if chunk > 0:
                    product = total[tile] + product
                if last:
                    rows.append(pressure(product))
                else:
                    total[tile] = product
            if last:
                for u in range(UNROLL // 2):
                    both = jnp.concatenate([rows[2 * u], rows[2 * u + 1]], axis=0)
                    partial[step * (UNROLL // 2) + u] = both.astype(jnp.bfloat16)
            if ahead:
                grow(slot, step)
            return carry

        lax.fori_loop(0, STEPS, contract, 0)

    own = pltpu.make_async_copy(partial.at[me], gathered.at[me], sum_recv)
    own.start()
    send_sums(STEPS - 1)
    pltpu.make_async_copy(gathered, gathered, sum_recv).wait()

    def add(i, carry):
        return carry + jnp.sum(gathered[pl.ds(i * 8, 8)].astype(jnp.float32), axis=0)

    summed = lax.fori_loop(0, FREQ_RANKS // 8, add, jnp.zeros((16, 128), jnp.float32))
    for blade in range(NCOMP):
        share_out[blade, 0:2, :] = summed[2 * blade : 2 * blade + 2, :]
        share_out[blade, 2:4, :] = summed[8 + 2 * blade : 8 + 2 * blade + 2, :]
        share_out[blade, 4:8, :] = jnp.zeros((4, 128), jnp.float32)
    for i in range(1, GRP_RANKS):
        other = (group + i) % GRP_RANKS
        pltpu.make_async_remote_copy(
            src_ref=share_out.at[other],
            dst_ref=share_in.at[group],
            send_sem=share_send,
            recv_sem=share_recv,
            device_id={"grp": other},
            device_id_type=MESH,
        ).start()
    pltpu.make_async_copy(share_out.at[group], share_in.at[group], share_recv).start()
    pltpu.make_async_copy(share_in, share_in, share_recv).wait()
    result = share_in[0] + share_in[1] + share_in[2] + share_in[3]
    for m in range(2):
        for j in range(JOINT):
            for part in range(2):
                out_ref[JOINT * m + j, part : part + 1, :] = result[
                    2 * m + part : 2 * m + part + 1, NOBS * j : NOBS * (j + 1)
                ]

    for chunk in range(CHUNKS):
        sent = received.at[chunk, pl.ds(0, ROWS * (FREQ_RANKS - 1)), :]
        pltpu.make_async_copy(sent, sent, send_sem.at[chunk]).wait()
    sent = gathered.at[pl.ds(0, FREQ_RANKS - 1)]
    pltpu.make_async_copy(sent, sent, sum_send).wait()
    sent = share_in.at[pl.ds(0, GRP_RANKS - 1)]
    pltpu.make_async_copy(sent, sent, share_send).wait()


def body(sources, panel_pos, panel_blade, observer_table, observer_index):
    me = lax.axis_index("freq")
    observers = jnp.tile(observer_table[:, observer_index], (1, JOINT))
    observers = jnp.pad(observers, ((0, 5), (0, 0)))
    position = lax.dynamic_slice_in_dim(panel_pos, me * SHARE, SHARE, 1)
    blade = lax.dynamic_slice_in_dim(panel_blade, me * SHARE, SHARE, 0).astype(jnp.float32)
    panels = jnp.concatenate([position, blade[None], jnp.zeros((4, SHARE), jnp.float32)], axis=0)
    bf16, f32 = jnp.bfloat16, jnp.float32
    dma = pltpu.SemaphoreType.DMA
    out = pl.pallas_call(
        kernel,
        out_shape=jax.ShapeDtypeStruct((8, 2, NOBS), f32),
        in_specs=[
            pl.BlockSpec(memory_space=pl.ANY),
            pl.BlockSpec(memory_space=pl.ANY),
            pl.BlockSpec(memory_space=pltpu.VMEM),
            pl.BlockSpec(memory_space=pltpu.VMEM),
        ],
        out_specs=pl.BlockSpec(memory_space=pltpu.VMEM),
        scratch_shapes=[
            pltpu.VMEM((ROWS, FREQ_RANKS * SHARE), bf16),
            pltpu.VMEM((2 * NF, NT), bf16),
            pltpu.VMEM((CHUNKS, NT, WIDTH), bf16),
            pltpu.VMEM((5, WIDTH, 128), f32),
            pltpu.VMEM((2, TILES, WIDTH, 256), bf16),
            pltpu.VMEM((TILES, 32, WIDTH), bf16),
            pltpu.VMEM((TILES, 32, 256), f32),
            pltpu.VMEM((FREQ_RANKS, 16, 128), bf16),
            pltpu.VMEM((FREQ_RANKS, 16, 128), bf16),
            pltpu.VMEM((NCOMP, 8, 128), f32),
            pltpu.VMEM((GRP_RANKS, 8, 128), f32),
            dma, dma, dma((CHUNKS,)), dma((CHUNKS,)), dma, dma, dma, dma,
        ],
        compiler_params=pltpu.CompilerParams(
            collective_id=0, has_side_effects=True, vmem_limit_bytes=60 * 2**20
        ),
    )(sources, transform_table(), panels, observers)
    return out[:, None]


def solution(mesh):
    in_specs = (P("freq", "grp"), P(None, "grp"), P("grp"), P(), P())
    out_specs = P("freq", "grp", None, None)
    return jax.shard_map(body, mesh=mesh, in_specs=in_specs, out_specs=out_specs, check_vma=False)
```

time: 452 us -> 86.2 us (0.19)
  the two profiles are of different devices: /device:TPU:1 before, /device:TPU:56 now
where the time goes in v1:
time: 86.2 us; the launch traced here: 85.9 us
  Pallas kernels  60.7 us (70%)
  other arithmetic  21.4 us (25%)
  local copies, waits for them, and re-layouts  3.85 us (4%)
    pallas_call x1, Pallas kernels, body(): pl.pallas_call(kernel, out_shape=jax.ShapeDtypeStruct((8, 2, NOBS), f32),...  60.7 us
    convert_element_type x1, other arithmetic, transform_table(): return (values / math.sqrt(NT)).astype(jnp.bfloat16)  19.2 us
    unnamed x4, local copies, waits for them, and re-layouts  2.41 us

profile of v1, /device:TPU:56, one launch (start us, length us, event | category | flops | bytes accessed | tf_op | source)
XLA Modules:
  0.0 85.9 jit_solution(12592242957000994676)
XLA Ops:
  0.0 0.0 copy-start
  0.0 0.7 compare_select_fusion
  0.8 0.1 pad.7.clone
  0.8 0.7 dynamic-slice_convert_fusion
  1.5 0.0 copy-done
  1.6 0.7 maximum_maximum_fusion.panel_ref
  2.2 1.1 %copy.6 = f32[3,2048]{0,1:T(8,128)S(1)} copy(f32[3,2048]{1,0:T(4,128)} %param.8) | data formatting | bytes 49152 | tf_op args[3]
  3.4 0.6 gather_fusion
  3.9 0.1 copy.7
  4.0 0.1 tile.10
  4.1 0.6 pad.4.observer_ref
  4.7 19.2 %multiply_convert_fusion.table_hbm = bf16[1024,1024]{1,0:T(8,128)(2,1)} fusion(s32[1024]{0:T(1024)S(1)} %fusion.16, pred[1024]{0:T(1024)(128)(4,1)S(1)} %fusion.13), kind=kLoop, calls=%fused_computation.7 | loop fusion | flops 18874368 | bytes 2102272 | tf_op jit(solution)/shard_map/convert_element_type | solution.py:39
  23.9 60.7 %shard_map.55 = f32[8,2,32]{2,1,0:T(2,128)} custom-call(bf16[16,65536]{1,0:T(8,128)(2,1)} %source_hbm.1, bf16[1024,1024]{1,0:T(8,128)(2,1)} %multiply_convert_fusion.table_hbm, f32[8,1024]{1,0:T(8,128)} %maximum_maximum_fusion.panel_ref, f32[8,128]{1,0:T(8,128)} %pad.4.observer_ref), custom_call_target="tpu_custom_call" | custom-call | tf_op jit(solution)/shard_map/pallas_call | solution.py:295
  84.6 1.3 %copy.10 = f32[8,1,2,32]{3,2,1,0:T(2,128)} copy(f32[8,1,2,32]{3,2,1,0:T(2,128)} %bitcast.5) | data formatting | bytes 4096
  (6 shorter events, 0.0 us)
Async XLA Ops:
  0.0 1.5 %copy-start = (f32[3,65536]{1,0:T(4,128)S(1)}, f32[3,65536]{1,0:T(4,128)}, u32[]{:S(2)}) copy-start(f32[3,65536]{1,0:T(4,128)} %param.6) | copy-start | bytes 2359300

commit v2 on v1

v2 whole, which is shorter than its diff:
```python
import math

import jax
import jax.numpy as jnp
import numpy as np
from jax import lax
from jax.experimental import pallas as pl
from jax.experimental.pallas import tpu as pltpu
from jax.sharding import PartitionSpec as P

NT = 1024
NF = 512
NCOMP = 4
NOBS = 32

wave_step = 0.04

FREQ_RANKS = 64
GRP_RANKS = 4
ROWS = NT // FREQ_RANKS
CHUNKS = 4
WIDTH = 256
SHARE = CHUNKS * WIDTH
JOINT = 4
TILES = NF // JOINT
UNROLL = 16
STEPS = TILES // UNROLL
MESH = pl.DeviceIdType.MESH


def transform_table():
    row_index = np.arange(2 * NF, dtype=np.int32)
    samples = np.arange(NT, dtype=np.int32)
    frequency = row_index // 8 * JOINT + row_index % JOINT
    parity = row_index // JOINT % 2
    turn_count = frequency[:, None] * samples[None, :] % NT
    angle_table = np.float32(2.0 * math.pi / NT) * turn_count.astype(np.float32)
    values = np.where(parity[:, None] == 0, np.cos(angle_table), -np.sin(angle_table))
    return (values / np.float32(math.sqrt(NT))).astype(jnp.bfloat16)


def kernel(
    source_hbm, table_hbm, position_hbm, blade_hbm, observers_hbm, index_hbm, out_ref,
    source, table, position, blade, observers, index, near, received, state, green_a, green_b, green_c, weighted, total,
    partial, gathered, share_out, share_in,
    load_sem, table_sem, small_sem, send_sem, recv_sem, sum_send, sum_recv, share_send, share_recv,
    x_sem, y_sem, group_sem,
):
    me = lax.axis_index("freq")
    group = lax.axis_index("grp")
    core, x, y, z = lax.rem(me, 2), lax.rem(lax.div(me, 2), 4), lax.rem(lax.div(me, 8), 4), lax.div(me, 32)
    xs = [2 * lax.rem(x + d, 4) for d in range(4)]
    ys = [8 * lax.rem(y + d, 4) for d in range(4)]
    zs = [32 * lax.rem(z + d // 2, 2) + lax.rem(core + d % 2, 2) for d in range(4)]
    along_x = [xs[d] + ys[0] + zs[0] for d in range(1, 4)]
    along_y = [xs[0] + ys[d] + zs[0] for d in range(1, 4)]
    along_z = [xs[0] + ys[0] + zs[d] for d in range(1, 4)]

    def signal(semaphore, device):
        pl.semaphore_signal(semaphore, inc=1, device_id={"freq": device}, device_id_type=MESH)

    def signal_groups(semaphore):
        for side in (1, GRP_RANKS - 1):
            other = lax.rem(group + side, GRP_RANKS)
            pl.semaphore_signal(semaphore, inc=1, device_id={"grp": other}, device_id_type=MESH)

    barrier = pltpu.get_barrier_semaphore()
    for device in along_x + along_y + along_z:
        signal(barrier, device)
    signal_groups(barrier)
    load = pltpu.make_async_copy(source_hbm, source, load_sem)
    load.start()
    share = pl.ds(pl.multiple_of(me * SHARE, SHARE), SHARE)
    small = [
        pltpu.make_async_copy(observers_hbm, observers, small_sem.at[0]),
        pltpu.make_async_copy(index_hbm, index, small_sem.at[1]),
        pltpu.make_async_copy(position_hbm.at[:, share], position, small_sem.at[2]),
        pltpu.make_async_copy(blade_hbm.at[pl.ds(pl.multiple_of(me * 8, 8), 8), :], blade, small_sem.at[3]),
    ]
    for copy in small:
        copy.start()
    table_load = pltpu.make_async_copy(table_hbm, table, table_sem)
    table_load.start()

    own_rows = pl.ds(pl.multiple_of(me * ROWS, ROWS), ROWS)

    def columns(device, chunk):
        return pl.ds(pl.multiple_of(device * SHARE + chunk * WIDTH, WIDTH), WIDTH)

    def send(device, chunk):
        pltpu.make_async_remote_copy(
            src_ref=source.at[:, columns(device, chunk)],
            dst_ref=received.at[chunk, own_rows, :],
            send_sem=send_sem.at[chunk],
            recv_sem=recv_sem.at[chunk],
            device_id={"freq": device},
            device_id_type=MESH,
        ).start()

    def seed(chunk):
        for half in range(WIDTH // 128):
            squares = None
            for axis in range(3):
                row = position[axis : axis + 1, pl.ds(chunk * WIDTH + half * 128, 128)]
                column = jnp.broadcast_to(row, (128, 128)).T
                offset = near[axis : axis + 1, :] - column
                squares = offset * offset if squares is None else squares + offset * offset
            inverse = lax.rsqrt(squares)
            distance = squares * inverse
            amplitude = (0.25 / math.pi) * inverse
            angle = wave_step * distance
            w = angle * angle
            cos1 = 1.0 + w * (-1 / 2 + w * (1 / 24 + w * (-1 / 720 + w * (1 / 40320 - w * (1 / 3628800)))))
            sin1 = angle * (1.0 + w * (-1 / 6 + w * (1 / 120 + w * (-1 / 5040 + w * (1 / 362880)))))
            cos2 = cos1 * cos1 - sin1 * sin1
            sin2 = 2.0 * sin1 * cos1
            cos3 = cos2 * cos1 - sin2 * sin1
            sin3 = sin2 * cos1 + cos2 * sin1
            cos4 = cos2 * cos2 - sin2 * sin2
            sin4 = 2.0 * sin2 * cos2
            lane = lax.broadcasted_iota(jnp.int32, (128, 128), 1) // NOBS
            cos_j = jnp.where(lane == 0, 1.0, jnp.where(lane == 1, cos1, jnp.where(lane == 2, cos2, cos3)))
            sin_j = jnp.where(lane == 0, 0.0, jnp.where(lane == 1, sin1, jnp.where(lane == 2, sin2, sin3)))
            rows = pl.ds(half * 128, 128)
            state[0, rows, :] = 2.0 * cos4
            state[1, rows, :] = amplitude * (cos_j * cos4 + sin_j * sin4)
            state[2, rows, :] = amplitude * cos_j
            state[3, rows, :] = -amplitude * (sin_j * cos4 - cos_j * sin4)
            state[4, rows, :] = -amplitude * sin_j

    load.wait()
    pl.semaphore_wait(barrier, 11)
    for device in along_x:
        signal(x_sem, device)
    signal_groups(group_sem)
    for d in range(3):
        for device in (along_x[d], along_y[d], along_z[d]):
            send(device, 0)
    for chunk in range(CHUNKS):
        pltpu.make_async_copy(
            source.at[:, columns(me, chunk)],
            received.at[chunk, own_rows, :],
            recv_sem.at[chunk],
        ).start()
    pl.semaphore_wait(x_sem, 3)
    for device in along_y:
        signal(y_sem, device)
    for d in range(1, 4):
        for e in range(1, 4):
            send(xs[(d + e) % 3 + 1] + ys[e] + zs[0], 0)
            send(xs[(d + e) % 3 + 1] + ys[0] + zs[e], 0)
    for copy in small:
        copy.wait()

    places = lax.broadcasted_iota(jnp.int32, (3, 2048), 1)
    lanes = lax.broadcasted_iota(jnp.int32, (3, 128), 1)
    whole = observers[...]
    chosen = jnp.zeros((3, 128), jnp.float32)
    for i in range(NOBS):
        picked = jnp.sum(jnp.where(places == index[i], whole, 0.0), axis=1, keepdims=True)
        chosen = jnp.where(lanes % NOBS == i, picked, chosen)
    near[...] = chosen

    pl.semaphore_wait(y_sem, 3)
    for d in range(4):
        for e in range(9):
            send(xs[(d + e) % 4] + ys[e // 3 + 1] + zs[e % 3 + 1], 0)
    seed(0)

    def send_some(step, chunk):
        turned = [2 * lax.rem(x + step + d, 4) for d in range(4)]
        half = lax.div(step, 4)
        lines = [8 * lax.rem(y + 2 * half + d, 4) for d in range(2)]
        for t in range(8):
            device = turned[t % 4] + lines[t // 4] + zs[(t + t // 4) % 4]
            if t == 0:
                pl.when(step > 0)(lambda: send(device, chunk))
            else:
                send(device, chunk)

    greens = (green_a, green_b, green_c, green_a)

    def grow(green, step, block):
        rows = pl.ds(block * 16, 16)
        twice = state[0, rows, :]
        re_old, re_new = state[1, rows, :], state[2, rows, :]
        im_old, im_new = state[3, rows, :], state[4, rows, :]
        for u in range(UNROLL):
            tile = step * UNROLL + u
            green[tile, rows, 0:128] = re_new.astype(jnp.bfloat16)
            green[tile, rows, 128:256] = im_new.astype(jnp.bfloat16)
            re_old, re_new = re_new, twice * re_new - re_old
            im_old, im_new = im_new, twice * im_new - im_old
        state[1, rows, :] = re_old
        state[2, rows, :] = re_new
        state[3, rows, :] = im_old
        state[4, rows, :] = im_new

    def grow_all(chunk, sent):
        def part(step, carry):
            if sent is not None:
                send_some(step, sent)
            for block in range(WIDTH // 16):
                grow(greens[chunk], step, block)
            return carry

        lax.fori_loop(0, STEPS, part, 0)

    grow_all(0, 1)
    seed(1)
    grow_all(1, None)
    seed(2)
    grow_all(2, 2)
    table_load.wait()

    sublane = lax.broadcasted_iota(jnp.int32, (8, 128), 0)
    lane_joint = lax.broadcasted_iota(jnp.int32, (8, 128), 1) // NOBS
    keep_a = (sublane == lane_joint).astype(jnp.float32)
    keep_c = (sublane == lane_joint + JOINT).astype(jnp.float32)

    def transform(chunk):
        blades = jnp.concatenate([blade[2 * chunk : 2 * chunk + 1, :], blade[2 * chunk + 1 : 2 * chunk + 2, :]], axis=1)
        masks = [(blades == b).astype(jnp.float32).reshape(1, 1, WIDTH) for b in range(NCOMP)]

        def part(i, carry):
            spectrum = jnp.dot(
                table[pl.ds(pl.multiple_of(i * 256, 256), 256), :],
                received[chunk],
                preferred_element_type=jnp.float32,
            ).reshape(32, 8, WIDTH)
            for pair in range(NCOMP // 2):
                both = jnp.concatenate([spectrum * masks[2 * pair], spectrum * masks[2 * pair + 1]], axis=1)
                weighted[pl.ds(i * 32, 32), pl.ds(16 * pair, 16), :] = both.astype(jnp.bfloat16)
            return carry

        lax.fori_loop(0, 4, part, 0)

    def pressure(value):
        sums = []
        for blade in range(NCOMP):
            re_side = value[8 * blade : 8 * blade + 8, 0:128]
            im_side = value[8 * blade : 8 * blade + 8, 128:256]
            sums.append(jnp.sum(re_side * keep_a - im_side * keep_c, axis=0, keepdims=True))
            sums.append(jnp.sum(im_side * keep_a + re_side * keep_c, axis=0, keepdims=True))
        return jnp.concatenate(sums, axis=0)

    def far_first(step):
        t = lax.rem(step, 4)
        line = lax.rem(y + 2 - t + 3 * lax.div(t, 2) + 2 * lax.div(t, 3), 4)
        return lax.rem(z + 1 - lax.div(step, 4), 2) * 4 + line

    def send_sums(step):
        for u in range(UNROLL // 2):
            device = far_first(step) * (UNROLL // 2) + u

            @pl.when(device != me)
            def _():
                pltpu.make_async_remote_copy(
                    src_ref=partial.at[device],
                    dst_ref=gathered.at[me],
                    send_sem=sum_send,
                    recv_sem=sum_recv,
                    device_id={"freq": device},
                    device_id_type=MESH,
                ).start()

    for chunk in range(CHUNKS):
        pltpu.make_async_copy(received.at[chunk], received.at[chunk], recv_sem.at[chunk]).wait()
        transform(chunk)
        last = chunk == CHUNKS - 1
        if chunk == 1:
            seed(3)

        def contract(step, carry):
            if chunk == 0:
                send_some(step, 3)
            if last:

                @pl.when(step > 0)
                def _():
                    send_sums(step - 1)

            rows = []
            place = far_first(step) if last else step
            for u in range(UNROLL):
                tile = place * UNROLL + u
                product = jnp.dot(weighted[tile], greens[chunk][tile], preferred_element_type=jnp.float32)
                if chunk > 0:
                    product = total[tile] + product
                if last:
                    rows.append(pressure(product))
                else:
                    total[tile] = product
                if chunk == 1:
                    grow(greens[3], step, u)
            if last:
                for u in range(UNROLL // 2):
                    both = jnp.concatenate([rows[2 * u], rows[2 * u + 1]], axis=0)
                    partial[place * (UNROLL // 2) + u] = both.astype(jnp.bfloat16)
            return carry

        lax.fori_loop(0, STEPS, contract, 0)

    own = pltpu.make_async_copy(partial.at[me], gathered.at[me], sum_recv)
    own.start()
    send_sums(STEPS - 1)
    pltpu.make_async_copy(gathered, gathered, sum_recv).wait()

    def add(i, carry):
        return carry + jnp.sum(gathered[pl.ds(i * 8, 8)].astype(jnp.float32), axis=0)

    summed = lax.fori_loop(0, FREQ_RANKS // 8, add, jnp.zeros((16, 128), jnp.float32))
    for blade in range(NCOMP):
        share_out[blade, 0:2, :] = summed[2 * blade : 2 * blade + 2, :]
        share_out[blade, 2:4, :] = summed[8 + 2 * blade : 8 + 2 * blade + 2, :]
        share_out[blade, 4:8, :] = jnp.zeros((4, 128), jnp.float32)
    pl.semaphore_wait(group_sem, 2)
    for i in range(1, GRP_RANKS):
        other = lax.rem(group + i, GRP_RANKS)
        pltpu.make_async_remote_copy(
            src_ref=share_out.at[other],
            dst_ref=share_in.at[group],
            send_sem=share_send,
            recv_sem=share_recv,
            device_id={"grp": other},
            device_id_type=MESH,
        ).start()
    pltpu.make_async_copy(share_out.at[group], share_in.at[group], share_recv).start()
    pltpu.make_async_copy(share_in, share_in, share_recv).wait()
    result = share_in[0] + share_in[1] + share_in[2] + share_in[3]
    for m in range(2):
        for j in range(JOINT):
            for part in range(2):
                out_ref[JOINT * m + j, 0, part : part + 1, :] = result[
                    2 * m + part : 2 * m + part + 1, NOBS * j : NOBS * (j + 1)
                ]

    for chunk in range(CHUNKS):
        sent = received.at[chunk, pl.ds(0, ROWS * (FREQ_RANKS - 1)), :]
        pltpu.make_async_copy(sent, sent, send_sem.at[chunk]).wait()
    sent = gathered.at[pl.ds(0, FREQ_RANKS - 1)]
    pltpu.make_async_copy(sent, sent, sum_send).wait()
    sent = share_in.at[pl.ds(0, GRP_RANKS - 1)]
    pltpu.make_async_copy(sent, sent, share_send).wait()


def body(sources, panel_pos, panel_blade, observer_table, observer_index):
    bf16, f32 = jnp.bfloat16, jnp.float32
    dma, regular = pltpu.SemaphoreType.DMA, pltpu.SemaphoreType.REGULAR
    out = pl.pallas_call(
        kernel,
        out_shape=jax.ShapeDtypeStruct((8, 1, 2, NOBS), f32),
        in_specs=[pl.BlockSpec(memory_space=pl.ANY)] * 6,
        out_specs=pl.BlockSpec(memory_space=pltpu.VMEM),
        scratch_shapes=[
            pltpu.VMEM((ROWS, FREQ_RANKS * SHARE), bf16),
            pltpu.VMEM((2 * NF, NT), bf16),
            pltpu.VMEM((3, SHARE), f32),
            pltpu.VMEM((8, 128), jnp.int32),
            pltpu.VMEM((3, 2048), f32),
            pltpu.SMEM((NOBS,), jnp.int32),
            pltpu.VMEM((3, 128), f32),
            pltpu.VMEM((CHUNKS, NT, WIDTH), bf16),
            pltpu.VMEM((5, WIDTH, 128), f32),
            pltpu.VMEM((TILES, WIDTH, 256), bf16),
            pltpu.VMEM((TILES, WIDTH, 256), bf16),
            pltpu.VMEM((TILES, WIDTH, 256), bf16),
            pltpu.VMEM((TILES, 32, WIDTH), bf16),
            pltpu.VMEM((TILES, 32, 256), f32),
            pltpu.VMEM((FREQ_RANKS, 16, 128), bf16),
            pltpu.VMEM((FREQ_RANKS, 16, 128), bf16),
            pltpu.VMEM((NCOMP, 8, 128), f32),
            pltpu.VMEM((GRP_RANKS, 8, 128), f32),
            dma, dma, dma((4,)), dma((CHUNKS,)), dma((CHUNKS,)), dma, dma, dma, dma,
            regular, regular, regular,
        ],
        compiler_params=pltpu.CompilerParams(
            collective_id=0, has_side_effects=True, vmem_limit_bytes=67043328
        ),
    )(sources, jnp.asarray(transform_table()), panel_pos, panel_blade.reshape(-1, 128), observer_table, observer_index)
    return out


def solution(mesh):
    in_specs = (P("freq", "grp"), P(None, "grp"), P("grp"), P(), P())
    out_specs = P("freq", "grp", None, None)
    return jax.shard_map(body, mesh=mesh, in_specs=in_specs, out_specs=out_specs, check_vma=False)
```

time: 86.2 us -> 56.6 us (0.66)
  the two profiles are of different devices: /device:TPU:56 before, /device:TPU:1 now
where the time goes in v2:
time: 56.6 us; the launch traced here: 56.4 us
  Pallas kernels  55.1 us (97%)
  local copies, waits for them, and re-layouts  1.3 us (2%)
    pallas_call x1, Pallas kernels, body(): pl.pallas_call(kernel, out_shape=jax.ShapeDtypeStruct((8, 1, 2, NOBS), f3...  55.1 us
    unnamed x1, local copies, waits for them, and re-layouts  1.3 us

profile of v2, /device:TPU:1, one launch (start us, length us, event | category | flops | bytes accessed | tf_op | source)
XLA Modules:
  0.0 56.4 jit_solution(5034335514160645416)
XLA Ops:
  0.0 55.1 %shard_map.64 = f32[8,1,2,32]{3,2,1,0:T(2,128)} custom-call(bf16[16,65536]{1,0:T(8,128)(2,1)} %source_hbm.1, bf16[1024,1024]{1,0:T(8,128)(2,1)} %constant.2.clone.table_hbm, f32[3,65536]{1,0:T(4,128)} %position_hbm.1, s32[512,128]{1,0:T(8,128)} %bitcast.1, f32[3,2048]{1,0:T(4,128)} %observers_hbm.1, s32[32]{0:T(128)} %index_hbm.1), custom_call_target="tpu_custom_call" | custom-call | tf_op jit(solution)/shard_map/pallas_call | solution.py:350
  55.1 1.3 %copy.8 = f32[8,1,2,32]{3,2,1,0:T(2,128)} copy(f32[8,1,2,32]{3,2,1,0:T(2,128)} %shard_map.64) | data formatting | bytes 4096

commit v3 on v2

--- a/solution.py
+++ b/solution.py
@@ -44,7 +44,7 @@
     source, table, position, blade, observers, index, near, received, state, green_a, green_b, green_c, weighted, total,
     partial, gathered, share_out, share_in,
     load_sem, table_sem, small_sem, send_sem, recv_sem, sum_send, sum_recv, share_send, share_recv,
-    x_sem, y_sem, group_sem,
+    group_sem,
 ):
     me = lax.axis_index("freq")
     group = lax.axis_index("grp")
@@ -52,10 +52,6 @@
     xs = [2 * lax.rem(x + d, 4) for d in range(4)]
     ys = [8 * lax.rem(y + d, 4) for d in range(4)]
     zs = [32 * lax.rem(z + d // 2, 2) + lax.rem(core + d % 2, 2) for d in range(4)]
-    along_x = [xs[d] + ys[0] + zs[0] for d in range(1, 4)]
-    along_y = [xs[0] + ys[d] + zs[0] for d in range(1, 4)]
-    along_z = [xs[0] + ys[0] + zs[d] for d in range(1, 4)]
-
     def signal(semaphore, device):
         pl.semaphore_signal(semaphore, inc=1, device_id={"freq": device}, device_id_type=MESH)
 
@@ -64,12 +60,12 @@
             other = lax.rem(group + side, GRP_RANKS)
             pl.semaphore_signal(semaphore, inc=1, device_id={"grp": other}, device_id_type=MESH)
 
-    barrier = pltpu.get_barrier_semaphore()
-    for device in along_x + along_y + along_z:
-        signal(barrier, device)
-    signal_groups(barrier)
     load = pltpu.make_async_copy(source_hbm, source, load_sem)
     load.start()
+    barrier = pltpu.get_barrier_semaphore()
+    for t in range(63, 0, -1):
+        signal(barrier, xs[t % 4] + ys[t // 4 % 4] + zs[t // 16])
+    signal_groups(barrier)
     share = pl.ds(pl.multiple_of(me * SHARE, SHARE), SHARE)
     small = [
         pltpu.make_async_copy(observers_hbm, observers, small_sem.at[0]),
@@ -128,27 +124,6 @@
             state[3, rows, :] = -amplitude * (sin_j * cos4 - cos_j * sin4)
             state[4, rows, :] = -amplitude * sin_j
 
-    load.wait()
-    pl.semaphore_wait(barrier, 11)
-    for device in along_x:
-        signal(x_sem, device)
-    signal_groups(group_sem)
-    for d in range(3):
-        for device in (along_x[d], along_y[d], along_z[d]):
-            send(device, 0)
-    for chunk in range(CHUNKS):
-        pltpu.make_async_copy(
-            source.at[:, columns(me, chunk)],
-            received.at[chunk, own_rows, :],
-            recv_sem.at[chunk],
-        ).start()
-    pl.semaphore_wait(x_sem, 3)
-    for device in along_y:
-        signal(y_sem, device)
-    for d in range(1, 4):
-        for e in range(1, 4):
-            send(xs[(d + e) % 3 + 1] + ys[e] + zs[0], 0)
-            send(xs[(d + e) % 3 + 1] + ys[0] + zs[e], 0)
     for copy in small:
         copy.wait()
 
@@ -161,12 +136,16 @@
         chosen = jnp.where(lanes % NOBS == i, picked, chosen)
     near[...] = chosen
 
-    pl.semaphore_wait(y_sem, 3)
-    for d in range(4):
-        for e in range(9):
-            send(xs[(d + e) % 4] + ys[e // 3 + 1] + zs[e % 3 + 1], 0)
     seed(0)
-
+    load.wait()
+    pl.semaphore_wait(barrier, 65)
+    signal_groups(group_sem)
+    for chunk in range(CHUNKS):
+        pltpu.make_async_copy(
+            source.at[:, columns(me, chunk)],
+            received.at[chunk, own_rows, :],
+            recv_sem.at[chunk],
+        ).start()
     def send_some(step, chunk):
         turned = [2 * lax.rem(x + step + d, 4) for d in range(4)]
         half = lax.div(step, 4)
@@ -206,11 +185,12 @@
 
         lax.fori_loop(0, STEPS, part, 0)
 
+    lax.fori_loop(0, 8, lambda step, c: (send_some(step, 0), c)[1], 0)
     grow_all(0, 1)
     seed(1)
-    grow_all(1, None)
+    grow_all(1, 2)
     seed(2)
-    grow_all(2, 2)
+    grow_all(2, 3)
     table_load.wait()
 
     sublane = lax.broadcasted_iota(jnp.int32, (8, 128), 0)
@@ -272,8 +252,6 @@
             seed(3)
 
         def contract(step, carry):
-            if chunk == 0:
-                send_some(step, 3)
             if last:
 
                 @pl.when(step > 0)
@@ -372,7 +350,7 @@
             pltpu.VMEM((NCOMP, 8, 128), f32),
             pltpu.VMEM((GRP_RANKS, 8, 128), f32),
             dma, dma, dma((4,)), dma((CHUNKS,)), dma((CHUNKS,)), dma, dma, dma, dma,
-            regular, regular, regular,
+            regular,
         ],
         compiler_params=pltpu.CompilerParams(
             collective_id=0, has_side_effects=True, vmem_limit_bytes=67043328

time: 56.6 us -> 54.6 us (0.965)
  Pallas kernels: 55.1 us -> 53.2 us
    pallas_call x1, Pallas kernels: 55.1 us -> 53.2 us  [body(): pl.pallas_call(kernel, out_shape=jax.ShapeDtypeStruct((8, 1, 2, NOBS), f3...]
where the time goes in v3:
time: 54.6 us; the launch traced here: 54.5 us
  Pallas kernels  53.2 us (97%)
  local copies, waits for them, and re-layouts  1.3 us (2%)
    pallas_call x1, Pallas kernels, body(): pl.pallas_call(kernel, out_shape=jax.ShapeDtypeStruct((8, 1, 2, NOBS), f3...  53.2 us
    unnamed x1, local copies, waits for them, and re-layouts  1.3 us

profile of v3, /device:TPU:1, one launch (start us, length us, event | category | flops | bytes accessed | tf_op | source)
XLA Modules:
  0.0 54.5 jit_solution(10147998495309541821)
XLA Ops:
  0.0 53.2 %shard_map.64 = f32[8,1,2,32]{3,2,1,0:T(2,128)} custom-call(bf16[16,65536]{1,0:T(8,128)(2,1)} %source_hbm.1, bf16[1024,1024]{1,0:T(8,128)(2,1)} %constant.2.clone.table_hbm, f32[3,65536]{1,0:T(4,128)} %position_hbm.1, s32[512,128]{1,0:T(8,128)} %bitcast.1, f32[3,2048]{1,0:T(4,128)} %observers_hbm.1, s32[32]{0:T(128)} %index_hbm.1), custom_call_target="tpu_custom_call" | custom-call | tf_op jit(solution)/shard_map/pallas_call | solution.py:328
  53.2 1.3 %copy.8 = f32[8,1,2,32]{3,2,1,0:T(2,128)} copy(f32[8,1,2,32]{3,2,1,0:T(2,128)} %shard_map.64) | data formatting | bytes 4096
